TPU v7x, 32 devices: a whole 2x2x4 slice. The times are simulated.
32 devices in a mesh: section: 2 (over y), dp: 16 (over z, x, core).
Axes of the slice: x: 2, y: 2, z: 4, core: 2. Of those that a mesh axis runs over, the one named last changes fastest.
Arguments:
- activations: bfloat16 [2, 8, 256, 3584], P('section', None, 'dp'), may hold values from -8 to 8
- cotangent: bfloat16 [2, 8, 256, 3584], P('section', None, 'dp'), may hold values from -96 to 96
- target_ids: int32 [8, 256], P(None, 'dp'), may hold values from -100 to 152063, as said below
- w_gate: bfloat16 [2, 3584, 96], P('section'), may hold values from -0.09375 to 0.09375
- w_up: bfloat16 [2, 3584, 96], P('section'), may hold values from -0.09375 to 0.09375
- w_down: bfloat16 [2, 96, 3584], P('section'), may hold values from -0.625 to 0.625
Outputs:
- grad_gate: float32 [2, 3584, 96], P('section', 'dp')
- grad_up: float32 [2, 3584, 96], P('section', 'dp')
- grad_down: float32 [2, 96, 3584], P('section', None, 'dp')
- grad_rms: float32 [], replicated
Inputs may be any that keep to these rules, and one draw needn't show every extreme that they name: `target_ids`: each entry is -100 (an ignored position) or a token id in 0 to 152063; the share of ignored positions differs between the blocks of 16 tokens of different replicas, from none to about eleven sixteenths.
All inputs are finite; a program needn't handle non-finite values.
Results may differ from a plain program's by a relative error of at most 0.0015.
Values sent between devices are 32-bit elements.
A program may use at most 64 MiB of HBM per device.

v0:
```python
import jax
import jax.numpy as jnp
from jax import lax
from jax.sharding import PartitionSpec as P


def own_rows(product, span, axis):
    everything = product(jnp.int32(0), lax.axis_size(axis) * span)
    own = lax.psum_scatter(everything, axis, scatter_dimension=0, tiled=True)
    return own


def finalize_totals(product):
    rounded = lax.optimization_barrier(product.astype(jnp.bfloat16))
    return jnp.sum(rounded.astype(jnp.float32), axis=0)


def combine_sums(values):
    replica_total = lax.psum(values, "dp")
    return lax.psum(replica_total, "section")


def shards(activations, cotangent, target_ids, w_gate, w_up, w_down):
    inputs_local = activations[0]
    valid = target_ids >= 0
    local_count = jnp.sum(valid.astype(jnp.float32))
    upstream = cotangent[0] * valid.astype(jnp.bfloat16)[:, :, None]
    gate_weight = w_gate[0]
    up_weight = w_up[0]
    down_weight = w_down[0]
    width = gate_weight.shape[1]
    model_width = inputs_local.shape[2]
    count = lax.psum(local_count, "dp")
    gate = jnp.einsum("mtd,dh->mth", inputs_local, gate_weight, preferred_element_type=jnp.float32)
    up = jnp.einsum("mtd,dh->mth", inputs_local, up_weight, preferred_element_type=jnp.float32)
    sigmoid_gate = jax.nn.sigmoid(gate)
    activated = gate * sigmoid_gate
    inner_activation = (activated * up).astype(jnp.bfloat16)
    hidden_grad = jnp.einsum(
        "mtd,hd->mth", upstream, down_weight, preferred_element_type=jnp.float32
    )
    gate_grad = (hidden_grad * up * sigmoid_gate * (1.0 + gate * (1.0 - sigmoid_gate))).astype(
        jnp.bfloat16
    )
    up_grad = (hidden_grad * activated).astype(jnp.bfloat16)

    def block_terms(start, count_rows):
        input_rows = lax.dynamic_slice_in_dim(inputs_local, start, count_rows, 2)
        incoming_gradient_lines = lax.dynamic_slice_in_dim(upstream, start, count_rows, 2)
        part_gate = finalize_totals(
            jnp.einsum("mtc,mth->mch", input_rows, gate_grad, preferred_element_type=jnp.float32)
        )
        part_up = finalize_totals(
            jnp.einsum("mtc,mth->mch", input_rows, up_grad, preferred_element_type=jnp.float32)
        )
        partial_lowering_weight = finalize_totals(
            jnp.einsum(
                "mth,mtc->mch",
                inner_activation,
                incoming_gradient_lines,
                preferred_element_type=jnp.float32,
            )
        )
        return jnp.concatenate([part_gate, part_up, partial_lowering_weight], axis=1)

    summed = own_rows(block_terms, model_width // lax.axis_size("dp"), "dp")
    entries = jnp.float32(lax.axis_size("section") * 3 * model_width * width)
    scaled = summed / count
    squares = jnp.sum(scaled * scaled)
    totals = combine_sums(squares[None])
    grad_rms = jnp.sqrt(totals[0] / entries)
    grad_gate = scaled[:, :width][None]
    grad_up = scaled[:, width : 2 * width][None]
    grad_down = jnp.transpose(scaled[:, 2 * width :])[None]
    return (grad_gate, grad_up, grad_down, grad_rms)


def solution(mesh):
    in_specs = (
        P("section", None, "dp", None),
        P("section", None, "dp", None),
        P(None, "dp"),
        P("section", None, None),
        P("section", None, None),
        P("section", None, None),
    )
    out_specs = (P("section", "dp", None), P("section", "dp", None), P("section", None, "dp"), P())
    return jax.shard_map(shards, mesh=mesh, in_specs=in_specs, out_specs=out_specs, check_vma=False)
```

profile of v0, /device:TPU:0, one launch (start us, length us, event | category | flops | bytes accessed | tf_op | source)
XLA Modules:
  0.0 160.1 jit_solution(7090689319286886474)
XLA Ops:
  7.2 0.0 copy-start
  7.2 0.0 reduce-scatter.4.cloned.1.call-start
  7.2 1.4 convert_reduce_fusion.3
  8.6 0.0 copy-done
  8.6 0.0 copy-start.1
  8.6 1.6 fusion.4
  10.2 1.5 fusion.6
  11.7 1.8 %fusion.8 = f32[8,16,96]{2,1,0:T(8,128)S(1)} fusion(bf16[1,8,16,3584]{3,2,1,0:T(8,128)(2,1)} %param.7, bf16[1,96,3584]{2,1,0:T(8,128)(2,1)} %param.11, bf16[8,16]{1,0:T(8,128)(2,1)S(1)} %convert_element_type.39), kind=kOutput, calls=%fused_computation.16 | convolution fusion | flops 88539136 | bytes 1655040 | tf_op jit(solution)/shard_map/mtd,hd->mth/dot_general | solution.py:39
  13.5 1.6 %fusion.1 = bf16[8,3584,96]{1,2,0:T(8,128)(2,1)S(1)} fusion(bf16[1,8,16,3584]{3,2,1,0:T(8,128)(2,1)S(1)} %copy-done, f32[8,16,96]{2,1,0:T(8,128)S(1)} %fusion.8, f32[8,16,96]{2,1,0:T(8,128)S(1)} %fusion.4), kind=kOutput, calls=%fused_computation.7 | convolution fusion | flops 90906624 | bytes 6520832 | tf_op jit(solution)/shard_map/mtc,mth->mch/dot_general | solution.py:54
  15.1 0.0 copy-done.1
  15.1 1.6 %convolution_convert_fusion = bf16[8,3584,96]{1,2,0:T(8,128)(2,1)S(1)} fusion(bf16[1,8,16,3584]{3,2,1,0:T(8,128)(2,1)S(1)} %copy-done.1, bf16[8,16]{1,0:T(8,128)(2,1)S(1)} %convert_element_type.39, f32[8,16,96]{2,1,0:T(8,128)S(1)} %fusion.6, f32[8,16,96]{2,1,0:T(8,128)S(1)} %fusion.4), kind=kOutput, calls=%fused_computation.3 | convolution fusion | flops 91365376 | bytes 6521088 | tf_op jit(solution)/shard_map/mth,mtc->mch/dot_general | solution.py:57
  16.8 1.6 %fusion = bf16[8,3584,96]{1,2,0:T(8,128)(2,1)S(1)} fusion(bf16[1,8,16,3584]{3,2,1,0:T(8,128)(2,1)S(1)} %copy-done, f32[8,16,96]{2,1,0:T(8,128)S(1)} %fusion.4, f32[8,16,96]{2,1,0:T(8,128)S(1)} %fusion.8, f32[8,16,96]{2,1,0:T(8,128)S(1)} %fusion.6), kind=kOutput, calls=%fused_computation.6 | convolution fusion | flops 90955776 | bytes 6569984 | tf_op jit(solution)/shard_map/mtc,mth->mch/dot_general | solution.py:51
  18.4 0.8 convert_reduce_fusion.2
  19.2 1.6 %convert_reduce_fusion = (f32[3584,96]{0,1:T(8,128)S(1)}, f32[3584,96]{0,1:T(8,128)S(1)}) fusion(bf16[8,3584,96]{1,2,0:T(8,128)(2,1)S(1)} %convolution_convert_fusion, bf16[8,3584,96]{1,2,0:T(8,128)(2,1)S(1)} %fusion.1), kind=kLoop, calls=%fused_computation | loop fusion | flops 10321920 | bytes 13762560 | tf_op jit(solution)/shard_map/reduce_sum | solution.py:15
  20.8 2.3 %pad_maximum_fusion = f32[3584,288]{0,1:T(8,128)} fusion(f32[3584,96]{0,1:T(8,128)S(1)} %get-tuple-element.11, f32[3584,96]{0,1:T(8,128)S(1)} %get-tuple-element.12, f32[3584,96]{0,1:T(8,128)S(1)} %convert_reduce_fusion.2), kind=kLoop, calls=%fused_computation.8 | loop fusion | flops 2064384 | bytes 8257536 | tf_op jit(solution)/shard_map/concatenate | solution.py:64
  23.1 5.8 %copy.10 = f32[3584,288]{1,0:T(8,128)} copy(f32[3584,288]{0,1:T(8,128)} %pad_maximum_fusion) | data formatting | bytes 8257536
  28.8 0.0 reduce-scatter.4.cloned.1.call-update
  28.9 35.7 %psum.21 = f32[]{:T(128)} all-reduce(f32[]{:T(128)} %get-tuple-element.6), channel_id=1, replica_groups=mesh['section'=2,'dp'=16] {'dp'}, use_global_device_ids=true, to_apply=%region_5.0 | all-reduce | flops 1 | bytes 8 | tf_op jit(solution)/shard_map/psum | solution.py:33
  64.5 47.1 %reduce-scatter.4.cloned.1.call-done = f32[224,288]{1,0:T(8,128)} async-done(((f32[3584,288]{1,0:T(8,128)}), f32[224,288]{1,0:T(8,128)}) %reduce-scatter.4.cloned.1.call-update) | async-done | bytes 258064
  111.7 1.1 copy.11
  112.8 1.3 multiply_reduce_fusion
  114.1 31.1 %psum.22 = f32[1]{0:T(128)} all-reduce(f32[1]{0:T(128)} %bitcast.15), channel_id=1, replica_groups=mesh['section'=2,'dp'=16] {'dp'}, use_global_device_ids=true, to_apply=%region_7.0 | all-reduce | flops 1 | bytes 8 | tf_op jit(solution)/shard_map/psum | solution.py:19
  145.2 0.7 slice_bitcast_fusion
  145.9 5.5 %psum.23 = f32[1]{0:T(128)} all-reduce(f32[1]{0:T(128)} %psum.22), channel_id=1, replica_groups=mesh['section'=2,'dp'=16] {'section'}, use_global_device_ids=true, to_apply=%region_8.0 | all-reduce | flops 1 | bytes 8 | tf_op jit(solution)/shard_map/psum | solution.py:20
  (1 shorter events, 0.0 us)
Async XLA Ops:
  7.2 1.4 copy-start
  7.2 104.5 %reduce-scatter.4.cloned.1.call-start = ((), (), s32[]{:S(2)}) async-start(), calls=%async_computation.1 | async-start | bytes 5849088
  8.6 6.5 %copy-start.1 = (bf16[1,8,16,3584]{3,2,1,0:T(8,128)(2,1)S(1)}, bf16[1,8,16,3584]{3,2,1,0:T(8,128)(2,1)}, u32[]{:S(2)}) copy-start(bf16[1,8,16,3584]{3,2,1,0:T(8,128)(2,1)} %param.7) | copy-start | bytes 2752516
Sparse Core Ops, SparseCore 0:
  29.0 82.6 reduce-scatter.3
where the time goes:
time: 161 us; the launch traced here: 160 us
  blocking collectives  72.3 us (45%)
  waiting for transfers between devices  47.1 us (29%)
  between operations  15.9 us (10%)
  matrix products  9.77 us (6%)
  local copies, waits for them, and re-layouts  7.61 us (5%)
  other arithmetic  7.33 us (5%)
    unnamed x2, waiting for transfers between devices  47.1 us
    psum x1, blocking collectives, shards(): count = lax.psum(local_count, 'dp')  35.7 us
    psum x1, blocking collectives, combine_sums(): replica_total = lax.psum(values, 'dp')  31.1 us
    unnamed x6, local copies, waits for them, and re-layouts  6.9 us
    psum x1, blocking collectives, combine_sums(): return lax.psum(replica_total, 'section')  5.54 us
  transfers between devices with their start and end apart: 1, of which 1 were waited for; matrix products, arithmetic and copies ran while one was open for 0% of the time, Pallas kernels for 0%

commit v1 on v0

--- a/solution.py
+++ b/solution.py
@@ -16,7 +16,11 @@
 
 
 def combine_sums(values):
-    replica_total = lax.psum(values, "dp")
+    replica_total = values
+    for hop in (1, 2, 4, 8):
+        replica_total = replica_total + lax.ppermute(
+            replica_total, "dp", [(dev, dev ^ hop) for dev in range(16)]
+        )
     return lax.psum(replica_total, "section")
 
 

time: 161 us -> 146 us (0.907)
  blocking collectives: 72.3 us -> 41.1 us
  starting transfers between devices: 0.04 us -> 8.32 us
  waiting for transfers between devices: 47.1 us -> 51.8 us
  between operations: 15.9 us -> 19.4 us
    psum x1 -> x0, blocking collectives: 31.1 us -> none  [combine_sums(): replica_total = lax.psum(values, 'dp')]
    ppermute x0 -> x4, starting transfers between devices: none -> 8.29 us  [combine_sums(): lax.ppermute(replica_total, 'dp', [(dev, dev ^ hop) for dev in range(16)])]
    ppermute x0 -> x4, waiting for transfers between devices: none -> 4.64 us  [combine_sums(): lax.ppermute(replica_total, 'dp', [(dev, dev ^ hop) for dev in range(16)])]
  transfers between devices with their start and end apart: 1 -> 5, of which waited for: 1 -> 5; matrix products, arithmetic and copies ran while one was open for 0% -> 0% of each run, Pallas kernels for 0% -> 0%
where the time goes in v1:
time: 146 us; the launch traced here: 145 us
  waiting for transfers between devices  51.8 us (35%)
  blocking collectives  41.1 us (28%)
  between operations  19.4 us (13%)
  matrix products  9.77 us (7%)
  starting transfers between devices  8.32 us (6%)
  local copies, waits for them, and re-layouts  7.61 us (5%)
  other arithmetic  7.33 us (5%)
    unnamed x2, waiting for transfers between devices  47.1 us
    psum x1, blocking collectives, shards(): count = lax.psum(local_count, 'dp')  35.7 us
    ppermute x4, starting transfers between devices, combine_sums(): lax.ppermute(replica_total, 'dp', [(dev, dev ^ hop) for dev in range(16)])  8.29 us
    unnamed x6, local copies, waits for them, and re-layouts  6.9 us
    psum x1, blocking collectives, combine_sums(): return lax.psum(replica_total, 'section')  5.42 us
    ppermute x4, waiting for transfers between devices, combine_sums(): lax.ppermute(replica_total, 'dp', [(dev, dev ^ hop) for dev in range(16)])  4.64 us
  transfers between devices with their start and end apart: 5, of which 5 were waited for; matrix products, arithmetic and copies ran while one was open for 0% of the time, Pallas kernels for 0%

profile of v1, /device:TPU:0, one launch (start us, length us, event | category | flops | bytes accessed | tf_op | source)
XLA Modules:
  0.0 145.3 jit_solution(10764215406235164392)
XLA Ops:
  7.2 0.0 copy-start
  7.2 0.0 reduce-scatter.4.cloned.1.call-start
  7.2 1.4 convert_reduce_fusion.3
  8.6 0.0 copy-done
  8.6 0.0 copy-start.1
  8.6 1.6 %fusion.4 = f32[8,16,96]{2,1,0:T(8,128)S(1)} fusion(bf16[1,8,16,3584]{3,2,1,0:T(8,128)(2,1)S(1)} %copy-done, bf16[1,3584,96]{1,2,0:T(8,128)(2,1)} %param.9), kind=kOutput, calls=%fused_computation.12 | convolution fusion | flops 88080384 | bytes 1654784 | tf_op jit(solution)/shard_map/mtd,dh->mth/dot_general | solution.py:38
  10.2 1.5 %fusion.6 = f32[8,16,96]{2,1,0:T(8,128)S(1)} fusion(bf16[1,8,16,3584]{3,2,1,0:T(8,128)(2,1)S(1)} %copy-done, bf16[1,3584,96]{1,2,0:T(8,128)(2,1)} %param.10), kind=kOutput, calls=%fused_computation.14 | convolution fusion | flops 88080384 | bytes 1654784 | tf_op jit(solution)/shard_map/mtd,dh->mth/dot_general | solution.py:39
  11.7 1.8 %fusion.8 = f32[8,16,96]{2,1,0:T(8,128)S(1)} fusion(bf16[1,8,16,3584]{3,2,1,0:T(8,128)(2,1)} %param.7, bf16[1,96,3584]{2,1,0:T(8,128)(2,1)} %param.11, bf16[8,16]{1,0:T(8,128)(2,1)S(1)} %convert_element_type.39), kind=kOutput, calls=%fused_computation.16 | convolution fusion | flops 88539136 | bytes 1655040 | tf_op jit(solution)/shard_map/mtd,hd->mth/dot_general | solution.py:43
  13.5 1.6 %fusion.1 = bf16[8,3584,96]{1,2,0:T(8,128)(2,1)S(1)} fusion(bf16[1,8,16,3584]{3,2,1,0:T(8,128)(2,1)S(1)} %copy-done, f32[8,16,96]{2,1,0:T(8,128)S(1)} %fusion.8, f32[8,16,96]{2,1,0:T(8,128)S(1)} %fusion.4), kind=kOutput, calls=%fused_computation.7 | convolution fusion | flops 90906624 | bytes 6520832 | tf_op jit(solution)/shard_map/mtc,mth->mch/dot_general | solution.py:58
  15.1 0.0 copy-done.1
  15.1 1.6 %convolution_convert_fusion = bf16[8,3584,96]{1,2,0:T(8,128)(2,1)S(1)} fusion(bf16[1,8,16,3584]{3,2,1,0:T(8,128)(2,1)S(1)} %copy-done.1, bf16[8,16]{1,0:T(8,128)(2,1)S(1)} %convert_element_type.39, f32[8,16,96]{2,1,0:T(8,128)S(1)} %fusion.6, f32[8,16,96]{2,1,0:T(8,128)S(1)} %fusion.4), kind=kOutput, calls=%fused_computation.3 | convolution fusion | flops 91365376 | bytes 6521088 | tf_op jit(solution)/shard_map/mth,mtc->mch/dot_general | solution.py:61
  16.8 1.6 %fusion = bf16[8,3584,96]{1,2,0:T(8,128)(2,1)S(1)} fusion(bf16[1,8,16,3584]{3,2,1,0:T(8,128)(2,1)S(1)} %copy-done, f32[8,16,96]{2,1,0:T(8,128)S(1)} %fusion.4, f32[8,16,96]{2,1,0:T(8,128)S(1)} %fusion.8, f32[8,16,96]{2,1,0:T(8,128)S(1)} %fusion.6), kind=kOutput, calls=%fused_computation.6 | convolution fusion | flops 90955776 | bytes 6569984 | tf_op jit(solution)/shard_map/mtc,mth->mch/dot_general | solution.py:55
  18.4 0.8 convert_reduce_fusion.2
  19.2 1.6 %convert_reduce_fusion = (f32[3584,96]{0,1:T(8,128)S(1)}, f32[3584,96]{0,1:T(8,128)S(1)}) fusion(bf16[8,3584,96]{1,2,0:T(8,128)(2,1)S(1)} %convolution_convert_fusion, bf16[8,3584,96]{1,2,0:T(8,128)(2,1)S(1)} %fusion.1), kind=kLoop, calls=%fused_computation | loop fusion | flops 10321920 | bytes 13762560 | tf_op jit(solution)/shard_map/reduce_sum | solution.py:15
  20.8 2.3 %pad_maximum_fusion = f32[3584,288]{0,1:T(8,128)} fusion(f32[3584,96]{0,1:T(8,128)S(1)} %get-tuple-element.11, f32[3584,96]{0,1:T(8,128)S(1)} %get-tuple-element.12, f32[3584,96]{0,1:T(8,128)S(1)} %convert_reduce_fusion.2), kind=kLoop, calls=%fused_computation.8 | loop fusion | flops 2064384 | bytes 8257536 | tf_op jit(solution)/shard_map/concatenate | solution.py:68
  23.1 5.8 %copy.10 = f32[3584,288]{1,0:T(8,128)} copy(f32[3584,288]{0,1:T(8,128)} %pad_maximum_fusion) | data formatting | bytes 8257536
  28.8 0.0 reduce-scatter.4.cloned.1.call-update
  28.9 35.7 %psum.14 = f32[]{:T(128)} all-reduce(f32[]{:T(128)} %get-tuple-element.6), channel_id=1, replica_groups=mesh['section'=2,'dp'=16] {'dp'}, use_global_device_ids=true, to_apply=%region_5.0 | all-reduce | flops 1 | bytes 8 | tf_op jit(solution)/shard_map/psum | solution.py:37
  64.5 47.1 %reduce-scatter.4.cloned.1.call-done = f32[224,288]{1,0:T(8,128)} async-done(((f32[3584,288]{1,0:T(8,128)}), f32[224,288]{1,0:T(8,128)}) %reduce-scatter.4.cloned.1.call-update) | async-done | bytes 258064
  111.7 1.1 copy.11
  112.8 1.3 multiply_reduce_fusion
  114.1 0.0 collective-permute-start
  114.1 1.3 collective-permute-done
  116.7 2.4 %collective-permute-start.1 = (f32[1]{0:T(128)}, f32[1]{0:T(128)}, u32[]{:S(2)}, u32[]{:S(2)}) collective-permute-start(f32[1]{0:T(128)} %add.26), channel_id=1, source_target_pairs={{0,2},{1,3},{2,0},{3,1},{4,6},{5,7},{6,4},{7,5},{8,10},{9,11},{10,... | collective-permute-start | bytes 20 | tf_op jit(solution)/shard_map/ppermute | solution.py:21
  119.1 1.2 collective-permute-done.1
  121.0 2.6 %collective-permute-start.2 = (f32[1]{0:T(128)}, f32[1]{0:T(128)}, u32[]{:S(2)}, u32[]{:S(2)}) collective-permute-start(f32[1]{0:T(128)} %add.27), channel_id=1, source_target_pairs={{0,4},{1,5},{2,6},{3,7},{4,0},{5,1},{6,2},{7,3},{8,12},{9,13},{10,... | collective-permute-start | bytes 20 | tf_op jit(solution)/shard_map/ppermute | solution.py:21
  123.6 1.0 collective-permute-done.2
  125.3 3.3 %collective-permute-start.3 = (f32[1]{0:T(128)}, f32[1]{0:T(128)}, u32[]{:S(2)}, u32[]{:S(2)}) collective-permute-start(f32[1]{0:T(128)} %add.28), channel_id=1, source_target_pairs={{0,8},{1,9},{2,10},{3,11},{4,12},{5,13},{6,14},{7,15},{8,0},{9,1},... | collective-permute-start | bytes 20 | tf_op jit(solution)/shard_map/ppermute | solution.py:21
  128.6 1.2 collective-permute-done.3
  130.5 0.7 slice_bitcast_fusion
  131.2 5.4 %psum.15 = f32[1]{0:T(128)} all-reduce(f32[1]{0:T(128)S(6)} %add.29), channel_id=1, replica_groups=mesh['section'=2,'dp'=16] {'section'}, use_global_device_ids=true, to_apply=%region_7.0 | all-reduce | flops 1 | bytes 8 | tf_op jit(solution)/shard_map/psum | solution.py:24
  (1 shorter events, 0.0 us)
Async XLA Ops:
  7.2 1.4 copy-start
  7.2 104.5 %reduce-scatter.4.cloned.1.call-start = ((), (), s32[]{:S(2)}) async-start(), calls=%async_computation.1 | async-start | bytes 5849088
  8.6 6.5 %copy-start.1 = (bf16[1,8,16,3584]{3,2,1,0:T(8,128)(2,1)S(1)}, bf16[1,8,16,3584]{3,2,1,0:T(8,128)(2,1)}, u32[]{:S(2)}) copy-start(bf16[1,8,16,3584]{3,2,1,0:T(8,128)(2,1)} %param.7) | copy-start | bytes 2752516
  114.1 1.3 collective-permute-start
  116.7 3.6 %collective-permute-start.1 = (f32[1]{0:T(128)}, f32[1]{0:T(128)}, u32[]{:S(2)}, u32[]{:S(2)}) collective-permute-start(f32[1]{0:T(128)} %add.26), channel_id=1, source_target_pairs={{0,2},{1,3},{2,0},{3,1},{4,6},{5,7},{6,4},{7,5},{8,10},{9,11},{10,... | collective-permute-start | bytes 20 | tf_op jit(solution)/shard_map/ppermute | solution.py:21
  121.0 3.6 %collective-permute-start.2 = (f32[1]{0:T(128)}, f32[1]{0:T(128)}, u32[]{:S(2)}, u32[]{:S(2)}) collective-permute-start(f32[1]{0:T(128)} %add.27), channel_id=1, source_target_pairs={{0,4},{1,5},{2,6},{3,7},{4,0},{5,1},{6,2},{7,3},{8,12},{9,13},{10,... | collective-permute-start | bytes 20 | tf_op jit(solution)/shard_map/ppermute | solution.py:21
  125.3 4.5 %collective-permute-start.3 = (f32[1]{0:T(128)}, f32[1]{0:T(128)}, u32[]{:S(2)}, u32[]{:S(2)}) collective-permute-start(f32[1]{0:T(128)} %add.28), channel_id=1, source_target_pairs={{0,8},{1,9},{2,10},{3,11},{4,12},{5,13},{6,14},{7,15},{8,0},{9,1},... | collective-permute-start | bytes 20 | tf_op jit(solution)/shard_map/ppermute | solution.py:21
Sparse Core Ops, SparseCore 0:
  29.0 82.6 reduce-scatter.3
